TPU v7x, 32 devices: a whole 2x2x4 slice. The times are simulated.
32 devices in a mesh: gx: 4 (over z), gy: 8 (over y, x, core).
Axes of the slice: x: 2, y: 2, z: 4, core: 2. Of those that a mesh axis runs over, the one named last changes fastest.
Arguments:
- gradient: float32 [32, 2048], P('gx', 'gy'), may hold values from -6 to 6
- warm_start: float32 [32, 2048], P('gx', 'gy'), may hold values from -3 to 3
- viscosity: float32 [32, 32, 2048], P(None, 'gx', 'gy'), may hold values from 1 to 10
- friction_coef: float32 [32, 2048], P('gx', 'gy'), may hold values from 0.5 to 5
- slide_dir: float32 [2, 32, 2048], P(None, 'gx', 'gy'), may hold values from -4 to 4
- obs_weight: float32 [32, 2048], P('gx', 'gy'), may hold values from 0.5 to 2
- ice_mask: int32 [32, 2048], P('gx', 'gy'), may hold values 0 or 1
- grounded: int32 [32, 2048], P('gx', 'gy'), may hold values 0 or 1
Outputs:
- solution: float32 [32, 2048], P('gx', 'gy')
- residual: float32 [32, 2048], P('gx', 'gy')
All inputs are finite; a program needn't handle non-finite values. No bound on the sum of `ice_mask` or of `grounded` on one device may be relied on, other than what follows from the above.
Results may differ from a plain program's by a relative error of at most 0.00075.
Values sent between devices are 32-bit elements; how exact they have to be, the bound alone decides.
A program may use at most 128 MiB of HBM per device.

v0:
```python
import jax
import jax.numpy as jnp
from jax import lax
from jax.sharding import PartitionSpec as P

ITERS = 2


vert_coupling = 128.0
sink_rate = 0.0625
bed_drag = 0.5
offset_weight = 0.0019
cross_share = 0.5
reg_gamma = 0.02
reg_smooth = 1.0
diag_scale = 0.003
neighbour_offsets = [
    (step_z, step_x, step_y)
    for step_z in (-1, 0, 1)
    for step_x in (-1, 0, 1)
    for step_y in (-1, 0, 1)
    if step_x != 0 or step_y != 0
]


def extended(block, sides, width):
    for axis, dim in sides:
        count = lax.axis_size(axis)
        forward = [(i, i + 1) for i in range(count - 1)]
        backward = [(target, source) for source, target in forward]
        low = lax.ppermute(
            lax.slice_in_dim(block, block.shape[dim] - width, None, axis=dim), axis, forward
        )
        high = lax.ppermute(lax.slice_in_dim(block, 0, width, axis=dim), axis, backward)
        block = jnp.concatenate([low, block, high], axis=dim)
    return block


def couple(field_ext, eta_ext):
    levels = eta_ext.shape[0]
    span_x = eta_ext.shape[1] - 2
    span_y = eta_ext.shape[2] - 2
    padded_field = jnp.pad(field_ext, ((0, 0), (1, 1), (0, 0), (0, 0)))
    padded_eta = jnp.pad(eta_ext, ((1, 1), (0, 0), (0, 0)))
    center = eta_ext[:, 1 : 1 + span_x, 1 : 1 + span_y]
    along_one = jnp.zeros((levels, span_x, span_y), jnp.float32)
    along_two = jnp.zeros((levels, span_x, span_y), jnp.float32)
    for step_z, step_x, step_y in neighbour_offsets:
        near_eta = padded_eta[
            1 + step_z : 1 + step_z + levels,
            1 + step_x : 1 + step_x + span_x,
            1 + step_y : 1 + step_y + span_y,
        ]
        weight = (
            offset_weight / (abs(step_x) + abs(step_y) + abs(step_z)) * 0.5 * (center + near_eta)
        )
        near_field = padded_field[
            :,
            1 + step_z : 1 + step_z + levels,
            1 + step_x : 1 + step_x + span_x,
            1 + step_y : 1 + step_y + span_y,
        ]
        along_one = along_one + weight * near_field[0]
        along_two = along_two + weight * near_field[1]
        if step_x != 0 and step_y != 0:
            twist_weight = cross_share * step_x * step_y * weight
            along_one = along_one + twist_weight * near_field[1]
            along_two = along_two + twist_weight * near_field[0]
    return jnp.stack([along_one, along_two])


def tridiagonal(link_weights, diagonal, rhs_cols):
    levels = diagonal.shape[0]
    pivot_value = diagonal[0]
    ratios = [-link_weights[0] / pivot_value]
    partial_value = [rhs_cols[:, 0] / pivot_value]
    for layer_index in range(1, levels):
        pivot_value = diagonal[layer_index] + link_weights[layer_index - 1] * ratios[-1]
        partial_value.append(
            (rhs_cols[:, layer_index] + link_weights[layer_index - 1] * partial_value[-1])
            / pivot_value
        )
        if layer_index < levels - 1:
            ratios.append(-link_weights[layer_index] / pivot_value)
    result = [partial_value[-1]]
    for layer_index in range(levels - 2, -1, -1):
        result.insert(0, partial_value[layer_index] - ratios[layer_index] * result[0])
    return jnp.stack(result, axis=1)


def responses(viscosity, friction):
    levels = viscosity.shape[0]
    link_weights = vert_coupling * 0.5 * (viscosity[:-1] + viscosity[1:])
    zero_layer = jnp.zeros_like(viscosity[:1])
    diagonal = (
        jnp.concatenate([zero_layer, link_weights])
        + jnp.concatenate([link_weights, zero_layer])
        + sink_rate * viscosity
    )
    diagonal = diagonal.at[0].add(bed_drag * friction)
    unit_rhs = jnp.zeros((2,) + viscosity.shape, jnp.float32)
    unit_rhs = unit_rhs.at[0, 0].set(1.0).at[1, levels - 1].set(1.0)
    solved = tridiagonal(link_weights, diagonal, unit_rhs)
    return (solved[0], solved[1])


def regularize(centre_ext):
    middle = centre_ext[1:-1, 1:-1]
    beside_all = (
        centre_ext[2:, 1:-1] + centre_ext[:-2, 1:-1] + centre_ext[1:-1, 2:] + centre_ext[1:-1, :-2]
    )
    return reg_gamma * (middle + reg_smooth * (4.0 * middle - beside_all))


def residual_dot(residual, precond):
    return lax.psum(jnp.sum(residual * precond), ("gx", "gy"))


def on_device(
    gradient, warm_start, viscosity, friction_coef, slide_dir, obs_weight, ice_mask, grounded
):
    ice_float = ice_mask.astype(jnp.float32)
    ground_float = grounded.astype(jnp.float32)
    friction = ground_float * friction_coef
    source = (ice_float * ground_float * friction_coef)[None] * slide_dir
    obs = ice_float * obs_weight
    inverse_diag = 1.0 / (
        reg_gamma * (1.0 + 4.0 * reg_smooth)
        + diag_scale * ice_float * ground_float * friction_coef * friction_coef
    )
    viscosity_wide = extended(viscosity, (("gx", 1), ("gy", 2)), 2)
    columns = jnp.concatenate([source, obs[None], friction[None]], axis=0)
    column_wide = extended(columns, (("gx", 1), ("gy", 2)), 2)
    safe_eta = jnp.where(viscosity_wide > 0.0, viscosity_wide, 1.0)
    bottom_wide, top_wide = responses(safe_eta, column_wide[3])
    bottom_inner = bottom_wide[:, 1:-1, 1:-1]
    top_inner = top_wide[:, 1:-1, 1:-1]
    bottom_own = bottom_wide[:, 2:-2, 2:-2]
    top_own = top_wide[:, 2:-2, 2:-2]

    def hessian(direction):
        wide_dir = extended(direction, (("gx", 0), ("gy", 1)), 2)
        spread = column_wide[:2] * wide_dir[None]
        first_state = bottom_wide[None] * spread[:, None]
        coupled = couple(first_state, viscosity_wide)
        surface = spread[:, 1:-1, 1:-1] * bottom_inner[-1][None] + jnp.sum(
            top_inner[None] * coupled, axis=1
        )
        traction = column_wide[2, 1:-1, 1:-1][None] * surface
        second_state = top_inner[None] * traction[:, None]
        coupled_back = couple(second_state, viscosity_wide[:, 1:-1, 1:-1])
        basal_part = traction[:, 1:-1, 1:-1] * top_own[0][None] + jnp.sum(
            bottom_own[None] * coupled_back, axis=1
        )
        return jnp.sum(source * basal_part, axis=0) + regularize(wide_dir[1:-1, 1:-1])

    solution = warm_start
    residual = gradient - hessian(warm_start)
    precond = inverse_diag * residual
    direction = precond
    norm_now = residual_dot(residual, precond)
    for iteration in range(ITERS):
        image_vec = hessian(direction)
        step_size = norm_now / lax.psum(jnp.sum(direction * image_vec), ("gx", "gy"))
        solution = solution + step_size * direction
        residual = residual - step_size * image_vec
        precond = inverse_diag * residual
        norm_next = residual_dot(residual, precond)
        direction = precond + norm_next / norm_now * direction
        norm_now = norm_next
    return (solution, residual)


def solution(mesh):
    return jax.shard_map(
        on_device,
        mesh=mesh,
        in_specs=(
            P("gx", "gy"),
            P("gx", "gy"),
            P(None, "gx", "gy"),
            P("gx", "gy"),
            P(None, "gx", "gy"),
            P("gx", "gy"),
            P("gx", "gy"),
            P("gx", "gy"),
        ),
        out_specs=(P("gx", "gy"), P("gx", "gy")),
        check_vma=False,
    )
```

profile of v0, /device:TPU:0, one launch (start us, length us, event | category | flops | bytes accessed | tf_op | source)
XLA Modules:
  0.0 328.0 jit_solution(8467789932187685515)
XLA Ops:
  1.4 4.9 %collective-permute-start.4 = (f32[2,256]{1,0:T(2,128)S(1)}, f32[2,256]{1,0:T(2,128)S(1)}, u32[]{:S(2)}, u32[]{:S(2)}) collective-permute-start(f32[2,256]{1,0:T(2,128)S(1)} %get-tuple-element.248), channel_id=1, source_target_pairs={{0,8},{8,16},{16,24},{1,9},{9,17},{17,25},{2,10},{10,18},{18,26},{... | collective-permute-start | bytes 6152 | tf_op jit(solution)/shard_map/ppermute | solution.py:31
  6.4 1.3 collective-permute-start.5
  9.2 4.7 %collective-permute-start = (f32[4,2,256]{2,1,0:T(2,128)S(1)}, f32[4,2,256]{2,1,0:T(2,128)S(1)}, u32[]{:S(2)}, u32[]{:S(2)}) collective-permute-start(f32[4,2,256]{2,1,0:T(2,128)S(1)} %get-tuple-element.233), channel_id=1, source_target_pairs={{0,8},{8,16},{16,24},{1,9},{9,17},{17,25},{2,10},{10,18},{18,26},{... | collective-permute-start | bytes 24584 | tf_op jit(solution)/shard_map/ppermute | solution.py:31
  13.8 1.3 collective-permute-start.1
  16.2 4.5 %collective-permute-start.8 = (f32[32,2,256]{2,1,0:T(2,128)S(1)}, f32[32,2,256]{2,1,0:T(2,128)S(1)}, u32[]{:S(2)}, u32[]{:S(2)}) collective-permute-start(f32[32,2,256]{2,1,0:T(2,128)S(1)} %get-tuple-element.229), channel_id=1, source_target_pairs={{0,8},{8,16},{16,24},{1,9},{9,17},{17,25},{2,10},{10,18},{18,26},{... | collective-permute-start | bytes 196616 | tf_op jit(solution)/shard_map/ppermute | solution.py:31
  20.8 1.3 collective-permute-start.9
  24.2 1.3 collective-permute-start.7
  25.6 4.8 %collective-permute-start.2 = (f32[4,12,2]{2,1,0:T(8,128)S(1)}, f32[4,12,2]{2,1,0:T(8,128)S(1)}, u32[]{:S(2)}, u32[]{:S(2)}) collective-permute-start(f32[4,12,2]{2,1,0:T(8,128)S(1)} %get-tuple-element.231), channel_id=1, source_target_pairs={{0,1},{1,2},{2,3},{3,4},{4,5},{5,6},{6,7},{8,9},{9,10},{10,11},{11... | collective-permute-start | bytes 1160 | tf_op jit(solution)/shard_map/ppermute | solution.py:31
  30.4 1.3 collective-permute-start.3
  32.5 2.2 collective-permute-done.3
  36.7 4.5 %collective-permute-start.10 = (f32[32,12,2]{2,1,0:T(8,128)S(1)}, f32[32,12,2]{2,1,0:T(8,128)S(1)}, u32[]{:S(2)}, u32[]{:S(2)}) collective-permute-start(f32[32,12,2]{2,1,0:T(8,128)S(1)} %get-tuple-element.225), channel_id=1, source_target_pairs={{0,1},{1,2},{2,3},{3,4},{4,5},{5,6},{6,7},{8,9},{9,10},{10,11},{11... | collective-permute-start | bytes 9224 | tf_op jit(solution)/shard_map/ppermute | solution.py:31
  41.2 1.3 collective-permute-start.11
  43.2 1.4 collective-permute-done.11
  51.7 9.6 %fusion.241 = (f32[1,32,10,258]{3,2,1,0:T(8,128)}, f32[32,10,258]{2,1,0:T(8,128)S(1)}, f32[32,10,258]{2,1,0:T(8,128)S(1)}, f32[32,10,258]{2,1,0:T(8,128)S(1)}, f...) fusion(f32[2,32,12,260]{3,2,1,0:T(8,128)S(1)} %broadcast_multip, ...), kind=kLoop, calls=%fused_computation.521 | loop fusion | flops 10815360 | bytes 27130368 | tf_op jit(solution)/shard_map/stack | solution.py:69
  61.4 9.7 %fusion.242 = f32[1,32,10,258]{3,2,1,0:T(8,128)} fusion(f32[32,10,258]{2,1,0:T(8,128)} %get-tuple-element.96, f32[32,10,258]{2,1,0:T(8,128)} %get-tuple-element.95, f32[32,10,258]{2,1,0:T(8,128)} %get-tuple-element.94, f32[32,10,258]{2,1,0:T(8,128)} %get-tuple-element.93, f32[32,10,258]{2,1,0:T(8,128)} %get-tuple-element.92, ...), kind=kLoop, calls=%fused_computation.522 | loop fusion | flops 7843200 | bytes 22459392 | tf_op jit(solution)/shard_map/stack | solution.py:69
  71.2 1.6 fusion
  74.4 4.4 %fusion.518 = (f32[1,32,8,256]{3,2,1,0:T(8,128)}, f32[32,8,256]{2,1,0:T(8,128)}, f32[32,8,256]{2,1,0:T(8,128)}, f32[32,8,256]{2,1,0:T(8,128)}, f32[32,8,256]{2,1...) fusion(f32[2,32,10,258]{3,2,1,0:T(8,128)S(1)} %broadcast_multip, ...), kind=kLoop, calls=%fused_computation.1103 | loop fusion | flops 8716288 | bytes 13500416 | tf_op jit(solution)/shard_map/stack | solution.py:69
  78.9 4.5 %fusion.515 = f32[1,32,8,256]{3,2,1,0:T(8,128)} fusion(f32[32,8,256]{2,1,0:T(8,128)} %get-tuple-element.71, f32[32,8,256]{2,1,0:T(8,128)} %get-tuple-element.70, f32[32,8,256]{2,1,0:T(8,128)} %get-tuple-element.69, f32[32,8,256]{2,1,0:T(8,128)} %get-tuple-element.68, f32[2,32,10,258]{3,2,1,0:T(8,128)S(1)} %broadcast_multiply_fusion.4, ...), kind=kLoop, calls=%fused_computation.1100 | loop fusion | flops 6619136 | bytes 11141120 | tf_op jit(solution)/shard_map/stack | solution.py:69
  85.7 1.6 fusion.594
  87.3 4.5 %collective-permute-start.12 = (f32[2,256]{1,0:T(2,128)S(1)}, f32[2,256]{1,0:T(2,128)S(1)}, u32[]{:S(2)}, u32[]{:S(2)}) collective-permute-start(f32[2,256]{1,0:T(2,128)S(1)} %get-tuple-element.246), channel_id=1, source_target_pairs={{0,8},{8,16},{16,24},{1,9},{9,17},{17,25},{2,10},{10,18},{18,26},{... | collective-permute-start | bytes 6152 | tf_op jit(solution)/shard_map/ppermute | solution.py:31
  91.9 1.3 collective-permute-start.13
  93.2 4.2 %collective-permute-done.13 = f32[2,256]{1,0:T(2,128)S(1)} collective-permute-done((f32[2,256]{1,0:T(2,128)S(1)}, f32[2,256]{1,0:T(2,128)S(1)}, u32[]{:S(2)}, u32[]{:S(2)}) %collective-permute-start.13) | collective-permute-done | bytes 2080 | tf_op jit(solution)/shard_map/ppermute | solution.py:34
  97.4 6.6 %collective-permute-start.14 = (f32[12,2]{1,0:T(8,128)S(1)}, f32[12,2]{1,0:T(8,128)S(1)}, u32[]{:S(2)}, u32[]{:S(2)}) collective-permute-start(f32[12,2]{1,0:T(8,128)S(1)} %get-tuple-element.237), channel_id=1, source_target_pairs={{0,1},{1,2},{2,3},{3,4},{4,5},{5,6},{6,7},{8,9},{9,10},{10,11},{11... | collective-permute-start | bytes 296 | tf_op jit(solution)/shard_map/ppermute | solution.py:31
  104.0 1.5 collective-permute-start.15
  105.5 2.5 collective-permute-done.15
  111.3 8.6 %fusion.244 = f32[1,32,10,258]{3,2,1,0:T(8,128)} fusion(f32[32,10,258]{2,1,0:T(8,128)} %get-tuple-element.96, f32[32,10,258]{2,1,0:T(8,128)} %get-tuple-element.95, f32[32,10,258]{2,1,0:T(8,128)} %get-tuple-element.94, f32[32,10,258]{2,1,0:T(8,128)} %get-tuple-element.93, f32[32,10,258]{2,1,0:T(8,128)} %get-tuple-element.92, ...), kind=kLoop, calls=%fused_computation.524 | loop fusion | flops 7843200 | bytes 22459392 | tf_op jit(solution)/shard_map/stack | solution.py:69
  120.0 8.6 %fusion.243 = f32[1,32,10,258]{3,2,1,0:T(8,128)} fusion(f32[32,10,258]{2,1,0:T(8,128)} %get-tuple-element.96, f32[32,10,258]{2,1,0:T(8,128)} %get-tuple-element.95, f32[32,10,258]{2,1,0:T(8,128)} %get-tuple-element.94, f32[32,10,258]{2,1,0:T(8,128)} %get-tuple-element.93, f32[32,10,258]{2,1,0:T(8,128)} %get-tuple-element.92, ...), kind=kLoop, calls=%fused_computation.523 | loop fusion | flops 7843200 | bytes 22459392 | tf_op jit(solution)/shard_map/stack | solution.py:69
  128.7 1.6 fusion.1
  131.1 4.5 %fusion.516 = f32[1,32,8,256]{3,2,1,0:T(8,128)} fusion(f32[32,8,256]{2,1,0:T(8,128)} %get-tuple-element.71, f32[32,8,256]{2,1,0:T(8,128)} %get-tuple-element.70, f32[32,8,256]{2,1,0:T(8,128)} %get-tuple-element.69, f32[32,8,256]{2,1,0:T(8,128)} %get-tuple-element.68, f32[2,32,10,258]{3,2,1,0:T(8,128)S(1)} %broadcast_multiply_fusion.2, ...), kind=kLoop, calls=%fused_computation.1101 | loop fusion | flops 6619136 | bytes 11141120 | tf_op jit(solution)/shard_map/stack | solution.py:69
  135.6 4.5 %fusion.519 = f32[1,32,8,256]{3,2,1,0:T(8,128)} fusion(f32[32,8,256]{2,1,0:T(8,128)} %get-tuple-element.71, f32[2,32,10,258]{3,2,1,0:T(8,128)S(1)} %broadcast_multiply_fusion.2, f32[32,8,256]{2,1,0:T(8,128)} %get-tuple-element.70, f32[32,8,256]{2,1,0:T(8,128)} %get-tuple-element.69, f32[32,8,256]{2,1,0:T(8,128)} %get-tuple-element.68, ...), kind=kLoop, calls=%fused_computation.1104 | loop fusion | flops 6619136 | bytes 11141120 | tf_op jit(solution)/shard_map/stack | solution.py:69
  142.2 1.5 multiply_reduce_fusion.2
  143.7 43.1 %all-reduce.10 = (f32[]{:T(128)}, f32[]{:T(128)}) all-reduce(f32[]{:T(128)} %get-tuple-element.39, f32[]{:T(128)} %get-tuple-element.38), channel_id=1, replica_groups=mesh['gx'=4,'gy'=8] {'gx','gy'}, use_global_device_ids=true, to_apply=%region_4.5 | all-reduce | flops 2 | bytes 16 | tf_op jit(solution)/shard_map/psum | solution.py:116
  188.2 2.0 multiply_reduce_fusion.1
  190.1 39.1 %psum.30 = f32[]{:T(128)} all-reduce(f32[]{:T(128)} %get-tuple-element.44), channel_id=1, replica_groups=mesh['gx'=4,'gy'=8] {'gx','gy'}, use_global_device_ids=true, to_apply=%region_11.12 | all-reduce | flops 1 | bytes 8 | tf_op jit(solution)/shard_map/psum | solution.py:116
  231.6 3.7 %collective-permute-start.16 = (f32[2,256]{1,0:T(2,128)S(1)}, f32[2,256]{1,0:T(2,128)S(1)}, u32[]{:S(2)}, u32[]{:S(2)}) collective-permute-start(f32[2,256]{1,0:T(2,128)S(1)} %get-tuple-element.244), channel_id=1, source_target_pairs={{0,8},{8,16},{16,24},{1,9},{9,17},{17,25},{2,10},{10,18},{18,26},{... | collective-permute-start | bytes 6152 | tf_op jit(solution)/shard_map/ppermute | solution.py:31
  235.3 1.3 collective-permute-start.17
  236.6 4.2 %collective-permute-done.17 = f32[2,256]{1,0:T(2,128)S(1)} collective-permute-done((f32[2,256]{1,0:T(2,128)S(1)}, f32[2,256]{1,0:T(2,128)S(1)}, u32[]{:S(2)}, u32[]{:S(2)}) %collective-permute-start.17) | collective-permute-done | bytes 2080 | tf_op jit(solution)/shard_map/ppermute | solution.py:34
  240.8 1.3 collective-permute-start.18
  242.1 1.5 collective-permute-start.19
  243.6 4.0 %collective-permute-done.19 = f32[12,2]{1,0:T(8,128)S(1)} collective-permute-done((f32[12,2]{1,0:T(8,128)S(1)}, f32[12,2]{1,0:T(8,128)S(1)}, u32[]{:S(2)}, u32[]{:S(2)}) %collective-permute-start.19) | collective-permute-done | bytes 128 | tf_op jit(solution)/shard_map/ppermute | solution.py:34
  250.5 8.8 %fusion.246 = f32[1,32,10,258]{3,2,1,0:T(8,128)} fusion(f32[32,10,258]{2,1,0:T(8,128)} %get-tuple-element.96, f32[32,10,258]{2,1,0:T(8,128)} %get-tuple-element.95, f32[32,10,258]{2,1,0:T(8,128)} %get-tuple-element.94, f32[32,10,258]{2,1,0:T(8,128)} %get-tuple-element.93, f32[32,10,258]{2,1,0:T(8,128)} %get-tuple-element.92, ...), kind=kLoop, calls=%fused_computation.526 | loop fusion | flops 7843200 | bytes 22003200 | tf_op jit(solution)/shard_map/stack | solution.py:69
  259.3 8.6 %fusion.245 = f32[1,32,10,258]{3,2,1,0:T(8,128)} fusion(f32[32,10,258]{2,1,0:T(8,128)} %get-tuple-element.96, f32[32,10,258]{2,1,0:T(8,128)} %get-tuple-element.95, f32[32,10,258]{2,1,0:T(8,128)} %get-tuple-element.94, f32[32,10,258]{2,1,0:T(8,128)} %get-tuple-element.93, f32[32,10,258]{2,1,0:T(8,128)} %get-tuple-element.92, ...), kind=kLoop, calls=%fused_computation.525 | loop fusion | flops 7843200 | bytes 22459392 | tf_op jit(solution)/shard_map/stack | solution.py:69
  268.0 1.6 fusion.2
  271.3 4.1 %fusion.517 = f32[1,32,8,256]{3,2,1,0:T(8,128)} fusion(f32[32,8,256]{2,1,0:T(8,128)} %get-tuple-element.71, f32[32,8,256]{2,1,0:T(8,128)} %get-tuple-element.70, f32[32,8,256]{2,1,0:T(8,128)} %get-tuple-element.69, f32[32,8,256]{2,1,0:T(8,128)} %get-tuple-element.68, f32[2,32,10,258]{3,2,1,0:T(8,128)S(1)} %broadcast_multiply_fusion, ...), kind=kLoop, calls=%fused_computation.1102 | loop fusion | flops 6619136 | bytes 11141120 | tf_op jit(solution)/shard_map/stack | solution.py:69
  275.4 4.0 %fusion.520 = f32[1,32,8,256]{3,2,1,0:T(8,128)} fusion(f32[32,8,256]{2,1,0:T(8,128)} %get-tuple-element.71, f32[2,32,10,258]{3,2,1,0:T(8,128)S(1)} %broadcast_multiply_fusion, f32[32,8,256]{2,1,0:T(8,128)} %get-tuple-element.70, f32[32,8,256]{2,1,0:T(8,128)} %get-tuple-element.69, f32[32,8,256]{2,1,0:T(8,128)} %get-tuple-element.68, ...), kind=kLoop, calls=%fused_computation.1105 | loop fusion | flops 6619136 | bytes 11141120 | tf_op jit(solution)/shard_map/stack | solution.py:69
  281.5 1.5 multiply_reduce_fusion
  283.0 42.3 %psum.31 = f32[]{:T(128)} all-reduce(f32[]{:T(128)} %get-tuple-element.42), channel_id=1, replica_groups=mesh['gx'=4,'gy'=8] {'gx','gy'}, use_global_device_ids=true, to_apply=%region_16.17 | all-reduce | flops 1 | bytes 8 | tf_op jit(solution)/shard_map/psum | solution.py:164
  326.7 1.3 multiply_subtract_fusion.30
  (246 shorter events, 33.0 us)
Async XLA Ops:
  1.4 19.4 %collective-permute-start.4 = (f32[2,256]{1,0:T(2,128)S(1)}, f32[2,256]{1,0:T(2,128)S(1)}, u32[]{:S(2)}, u32[]{:S(2)}) collective-permute-start(f32[2,256]{1,0:T(2,128)S(1)} %get-tuple-element.248), channel_id=1, source_target_pairs={{0,8},{8,16},{16,24},{1,9},{9,17},{17,25},{2,10},{10,18},{18,26},{... | collective-permute-start | bytes 6152 | tf_op jit(solution)/shard_map/ppermute | solution.py:31
  6.4 15.7 %collective-permute-start.5 = (f32[2,256]{1,0:T(2,128)S(1)}, f32[2,256]{1,0:T(2,128)S(1)}, u32[]{:S(2)}, u32[]{:S(2)}) collective-permute-start(f32[2,256]{1,0:T(2,128)S(1)} %get-tuple-element.249), channel_id=1, source_target_pairs={{8,0},{16,8},{24,16},{9,1},{17,9},{25,17},{10,2},{18,10},{26,18},{... | collective-permute-start | bytes 6152 | tf_op jit(solution)/shard_map/ppermute | solution.py:34
  8.4 132.9 %copy-start.48 = (f32[8,256]{1,0:T(8,128)}, f32[8,256]{1,0:T(8,128)S(1)}, u32[]{:S(2)}) copy-start(f32[8,256]{1,0:T(8,128)S(1)} %get-tuple-element.242) | copy-start | bytes 24580
  9.1 35.5 %copy-start.12 = (f32[32,8,256]{2,1,0:T(8,128)S(1)}, f32[32,8,256]{2,1,0:T(8,128)}, u32[]{:S(2)}) copy-start(f32[32,8,256]{2,1,0:T(8,128)} %param.16) | copy-start | bytes 786436
  9.2 15.0 %collective-permute-start = (f32[4,2,256]{2,1,0:T(2,128)S(1)}, f32[4,2,256]{2,1,0:T(2,128)S(1)}, u32[]{:S(2)}, u32[]{:S(2)}) collective-permute-start(f32[4,2,256]{2,1,0:T(2,128)S(1)} %get-tuple-element.233), channel_id=1, source_target_pairs={{0,8},{8,16},{16,24},{1,9},{9,17},{17,25},{2,10},{10,18},{18,26},{... | collective-permute-start | bytes 24584 | tf_op jit(solution)/shard_map/ppermute | solution.py:31
  13.8 11.7 %collective-permute-start.1 = (f32[4,2,256]{2,1,0:T(2,128)S(1)}, f32[4,2,256]{2,1,0:T(2,128)S(1)}, u32[]{:S(2)}, u32[]{:S(2)}) collective-permute-start(f32[4,2,256]{2,1,0:T(2,128)S(1)} %get-tuple-element.234), channel_id=1, source_target_pairs={{8,0},{16,8},{24,16},{9,1},{17,9},{25,17},{10,2},{18,10},{26,18},{... | collective-permute-start | bytes 24584 | tf_op jit(solution)/shard_map/ppermute | solution.py:34
  16.2 18.7 %collective-permute-start.8 = (f32[32,2,256]{2,1,0:T(2,128)S(1)}, f32[32,2,256]{2,1,0:T(2,128)S(1)}, u32[]{:S(2)}, u32[]{:S(2)}) collective-permute-start(f32[32,2,256]{2,1,0:T(2,128)S(1)} %get-tuple-element.229), channel_id=1, source_target_pairs={{0,8},{8,16},{16,24},{1,9},{9,17},{17,25},{2,10},{10,18},{18,26},{... | collective-permute-start | bytes 196616 | tf_op jit(solution)/shard_map/ppermute | solution.py:31
  20.8 24.5 %copy-start.59 = (f32[2,256]{1,0:T(2,128)}, f32[2,256]{1,0:T(2,128)S(1)}, u32[]{:S(2)}) copy-start(f32[2,256]{1,0:T(2,128)S(1)} %collective-permute-done.4) | copy-start | bytes 6148
  20.8 14.7 %collective-permute-start.9 = (f32[32,2,256]{2,1,0:T(2,128)S(1)}, f32[32,2,256]{2,1,0:T(2,128)S(1)}, u32[]{:S(2)}, u32[]{:S(2)}) collective-permute-start(f32[32,2,256]{2,1,0:T(2,128)S(1)} %get-tuple-element.230), channel_id=1, source_target_pairs={{8,0},{16,8},{24,16},{9,1},{17,9},{25,17},{10,2},{18,10},{26,18},{... | collective-permute-start | bytes 196616 | tf_op jit(solution)/shard_map/ppermute | solution.py:34
  22.1 23.2 %copy-start.61 = (f32[2,256]{1,0:T(2,128)}, f32[2,256]{1,0:T(2,128)S(1)}, u32[]{:S(2)}) copy-start(f32[2,256]{1,0:T(2,128)S(1)} %collective-permute-done.5) | copy-start | bytes 6148
  22.9 7.5 %collective-permute-start.6 = (f32[12,2]{1,0:T(8,128)S(1)}, f32[12,2]{1,0:T(8,128)S(1)}, u32[]{:S(2)}, u32[]{:S(2)}) collective-permute-start(f32[12,2]{1,0:T(8,128)S(1)} %get-tuple-element.239), channel_id=1, source_target_pairs={{0,1},{1,2},{2,3},{3,4},{4,5},{5,6},{6,7},{8,9},{9,10},{10,11},{11... | collective-permute-start | bytes 296 | tf_op jit(solution)/shard_map/ppermute | solution.py:31
  24.2 7.5 %collective-permute-start.7 = (f32[12,2]{1,0:T(8,128)S(1)}, f32[12,2]{1,0:T(8,128)S(1)}, u32[]{:S(2)}, u32[]{:S(2)}) collective-permute-start(f32[12,2]{1,0:T(8,128)S(1)} %get-tuple-element.240), channel_id=1, source_target_pairs={{1,0},{2,1},{3,2},{4,3},{5,4},{6,5},{7,6},{9,8},{10,9},{11,10},{12... | collective-permute-start | bytes 296 | tf_op jit(solution)/shard_map/ppermute | solution.py:34
  25.6 6.9 %collective-permute-start.2 = (f32[4,12,2]{2,1,0:T(8,128)S(1)}, f32[4,12,2]{2,1,0:T(8,128)S(1)}, u32[]{:S(2)}, u32[]{:S(2)}) collective-permute-start(f32[4,12,2]{2,1,0:T(8,128)S(1)} %get-tuple-element.231), channel_id=1, source_target_pairs={{0,1},{1,2},{2,3},{3,4},{4,5},{5,6},{6,7},{8,9},{9,10},{10,11},{11... | collective-permute-start | bytes 1160 | tf_op jit(solution)/shard_map/ppermute | solution.py:31
  30.4 14.9 %copy-start.57 = (f32[12,2]{1,0:T(8,128)}, f32[12,2]{1,0:T(8,128)S(1)}, u32[]{:S(2)}) copy-start(f32[12,2]{1,0:T(8,128)S(1)} %collective-permute-done.6) | copy-start | bytes 292
  30.4 4.3 %collective-permute-start.3 = (f32[4,12,2]{2,1,0:T(8,128)S(1)}, f32[4,12,2]{2,1,0:T(8,128)S(1)}, u32[]{:S(2)}, u32[]{:S(2)}) collective-permute-start(f32[4,12,2]{2,1,0:T(8,128)S(1)} %get-tuple-element.232), channel_id=1, source_target_pairs={{1,0},{2,1},{3,2},{4,3},{5,4},{6,5},{7,6},{9,8},{10,9},{11,10},{12... | collective-permute-start | bytes 1160 | tf_op jit(solution)/shard_map/ppermute | solution.py:34
  31.7 13.6 %copy-start.58 = (f32[12,2]{1,0:T(8,128)}, f32[12,2]{1,0:T(8,128)S(1)}, u32[]{:S(2)}) copy-start(f32[12,2]{1,0:T(8,128)S(1)} %collective-permute-done.7) | copy-start | bytes 292
  34.9 16.2 %copy-start.32 = (f32[2,12,260]{2,1,0:T(8,128)}, f32[2,12,260]{2,1,0:T(8,128)S(1)}, u32[]{:S(2)}) copy-start(f32[2,12,260]{2,1,0:T(8,128)S(1)} %slice_multiply_fusion.5) | copy-start | bytes 74884
  36.7 6.5 %collective-permute-start.10 = (f32[32,12,2]{2,1,0:T(8,128)S(1)}, f32[32,12,2]{2,1,0:T(8,128)S(1)}, u32[]{:S(2)}, u32[]{:S(2)}) collective-permute-start(f32[32,12,2]{2,1,0:T(8,128)S(1)} %get-tuple-element.225), channel_id=1, source_target_pairs={{0,1},{1,2},{2,3},{3,4},{4,5},{5,6},{6,7},{8,9},{9,10},{10,11},{11... | collective-permute-start | bytes 9224 | tf_op jit(solution)/shard_map/ppermute | solution.py:31
  41.2 3.4 %collective-permute-start.11 = (f32[32,12,2]{2,1,0:T(8,128)S(1)}, f32[32,12,2]{2,1,0:T(8,128)S(1)}, u32[]{:S(2)}, u32[]{:S(2)}) collective-permute-start(f32[32,12,2]{2,1,0:T(8,128)S(1)} %get-tuple-element.226), channel_id=1, source_target_pairs={{1,0},{2,1},{3,2},{4,3},{5,4},{6,5},{7,6},{9,8},{10,9},{11,10},{12... | collective-permute-start | bytes 9224 | tf_op jit(solution)/shard_map/ppermute | solution.py:34
  50.2 22.6 %copy-start.38 = (f32[10,258]{1,0:T(8,128)}, f32[10,258]{1,0:T(8,128)S(1)}, u32[]{:S(2)}) copy-start(f32[10,258]{1,0:T(8,128)S(1)} %slice_bitcast_fusion.98) | copy-start | bytes 30964
  51.7 9.6 %copy-start.13 = (f32[32,12,258]{2,1,0:T(8,128)}, f32[32,12,258]{2,1,0:T(8,128)S(1)}, u32[]{:S(2)}) copy-start(f32[32,12,258]{2,1,0:T(8,128)S(1)} %get-tuple-element.227) | copy-start | bytes 1188868
  51.7 9.6 %copy-start.15 = (f32[32,12,258]{2,1,0:T(8,128)}, f32[32,12,258]{2,1,0:T(8,128)S(1)}, u32[]{:S(2)}) copy-start(f32[32,12,258]{2,1,0:T(8,128)S(1)} %get-tuple-element.228) | copy-start | bytes 1188868
  61.3 9.8 %copy-start = (f32[32,10,258]{2,1,0:T(8,128)}, f32[32,10,258]{2,1,0:T(8,128)S(1)}, u32[]{:S(2)}) copy-start(f32[32,10,258]{2,1,0:T(8,128)S(1)} %get-tuple-element.76) | copy-start | bytes 990724
  61.3 9.8 %copy-start.3 = (f32[32,10,258]{2,1,0:T(8,128)}, f32[32,10,258]{2,1,0:T(8,128)S(1)}, u32[]{:S(2)}) copy-start(f32[32,10,258]{2,1,0:T(8,128)S(1)} %get-tuple-element.77) | copy-start | bytes 990724
  61.4 9.8 %copy-start.6 = (f32[32,10,258]{2,1,0:T(8,128)}, f32[32,10,258]{2,1,0:T(8,128)S(1)}, u32[]{:S(2)}) copy-start(f32[32,10,258]{2,1,0:T(8,128)S(1)} %get-tuple-element.78) | copy-start | bytes 990724
  61.4 9.8 %copy-start.9 = (f32[32,10,258]{2,1,0:T(8,128)}, f32[32,10,258]{2,1,0:T(8,128)S(1)}, u32[]{:S(2)}) copy-start(f32[32,10,258]{2,1,0:T(8,128)S(1)} %get-tuple-element.79) | copy-start | bytes 990724
  72.9 5.9 %copy-start.45 = (f32[2,10,258]{2,1,0:T(8,128)}, f32[2,10,258]{2,1,0:T(8,128)S(1)}, u32[]{:S(2)}) copy-start(f32[2,10,258]{2,1,0:T(8,128)S(1)} %fusion.526) | copy-start | bytes 61924
  78.9 5.8 %copy-start.47 = (f32[2,8,256]{2,1,0:T(8,128)S(1)}, f32[2,8,256]{2,1,0:T(8,128)}, u32[]{:S(2)}) copy-start(f32[2,8,256]{2,1,0:T(8,128)} %param.18) | copy-start | bytes 49156
  78.9 6.8 %copy-start.60 = (f32[2,256]{1,0:T(2,128)S(1)}, f32[2,256]{1,0:T(2,128)}, u32[]{:S(2)}) copy-start(f32[2,256]{1,0:T(2,128)} %copy-done.59) | copy-start | bytes 6148
  83.4 27.9 %copy-start.10 = (f32[32,10,258]{2,1,0:T(8,128)S(1)}, f32[32,10,258]{2,1,0:T(8,128)}, u32[]{:S(2)}) copy-start(f32[32,10,258]{2,1,0:T(8,128)} %copy-done.9) | copy-start | bytes 990724
  84.6 26.7 %copy-start.1 = (f32[32,10,258]{2,1,0:T(8,128)S(1)}, f32[32,10,258]{2,1,0:T(8,128)}, u32[]{:S(2)}) copy-start(f32[32,10,258]{2,1,0:T(8,128)} %copy-done) | copy-start | bytes 990724
  84.7 26.7 %copy-start.4 = (f32[32,10,258]{2,1,0:T(8,128)S(1)}, f32[32,10,258]{2,1,0:T(8,128)}, u32[]{:S(2)}) copy-start(f32[32,10,258]{2,1,0:T(8,128)} %copy-done.3) | copy-start | bytes 990724
  84.7 26.7 %copy-start.7 = (f32[32,10,258]{2,1,0:T(8,128)S(1)}, f32[32,10,258]{2,1,0:T(8,128)}, u32[]{:S(2)}) copy-start(f32[32,10,258]{2,1,0:T(8,128)} %copy-done.6) | copy-start | bytes 990724
  87.3 5.9 %collective-permute-start.12 = (f32[2,256]{1,0:T(2,128)S(1)}, f32[2,256]{1,0:T(2,128)S(1)}, u32[]{:S(2)}, u32[]{:S(2)}) collective-permute-start(f32[2,256]{1,0:T(2,128)S(1)} %get-tuple-element.246), channel_id=1, source_target_pairs={{0,8},{8,16},{16,24},{1,9},{9,17},{17,25},{2,10},{10,18},{18,26},{... | collective-permute-start | bytes 6152 | tf_op jit(solution)/shard_map/ppermute | solution.py:31
  91.9 5.5 %collective-permute-start.13 = (f32[2,256]{1,0:T(2,128)S(1)}, f32[2,256]{1,0:T(2,128)S(1)}, u32[]{:S(2)}, u32[]{:S(2)}) collective-permute-start(f32[2,256]{1,0:T(2,128)S(1)} %get-tuple-element.247), channel_id=1, source_target_pairs={{8,0},{16,8},{24,16},{9,1},{17,9},{25,17},{10,2},{18,10},{26,18},{... | collective-permute-start | bytes 6152 | tf_op jit(solution)/shard_map/ppermute | solution.py:34
  97.3 10.8 %copy-start.64 = (f32[2,256]{1,0:T(2,128)}, f32[2,256]{1,0:T(2,128)S(1)}, u32[]{:S(2)}) copy-start(f32[2,256]{1,0:T(2,128)S(1)} %collective-permute-done.13) | copy-start | bytes 6148
  97.4 8.1 %collective-permute-start.14 = (f32[12,2]{1,0:T(8,128)S(1)}, f32[12,2]{1,0:T(8,128)S(1)}, u32[]{:S(2)}, u32[]{:S(2)}) collective-permute-start(f32[12,2]{1,0:T(8,128)S(1)} %get-tuple-element.237), channel_id=1, source_target_pairs={{0,1},{1,2},{2,3},{3,4},{4,5},{5,6},{6,7},{8,9},{9,10},{10,11},{11... | collective-permute-start | bytes 296 | tf_op jit(solution)/shard_map/ppermute | solution.py:31
  104.0 4.0 %collective-permute-start.15 = (f32[12,2]{1,0:T(8,128)S(1)}, f32[12,2]{1,0:T(8,128)S(1)}, u32[]{:S(2)}, u32[]{:S(2)}) collective-permute-start(f32[12,2]{1,0:T(8,128)S(1)} %get-tuple-element.238), channel_id=1, source_target_pairs={{1,0},{2,1},{3,2},{4,3},{5,4},{6,5},{7,6},{9,8},{10,9},{11,10},{12... | collective-permute-start | bytes 296 | tf_op jit(solution)/shard_map/ppermute | solution.py:34
  230.6 19.9 %copy-start.2 = (f32[32,10,258]{2,1,0:T(8,128)S(1)}, f32[32,10,258]{2,1,0:T(8,128)}, u32[]{:S(2)}) copy-start(f32[32,10,258]{2,1,0:T(8,128)} %copy-done) | copy-start | bytes 990724
  230.6 19.9 %copy-start.5 = (f32[32,10,258]{2,1,0:T(8,128)S(1)}, f32[32,10,258]{2,1,0:T(8,128)}, u32[]{:S(2)}) copy-start(f32[32,10,258]{2,1,0:T(8,128)} %copy-done.3) | copy-start | bytes 990724
  230.6 19.9 %copy-start.8 = (f32[32,10,258]{2,1,0:T(8,128)S(1)}, f32[32,10,258]{2,1,0:T(8,128)}, u32[]{:S(2)}) copy-start(f32[32,10,258]{2,1,0:T(8,128)} %copy-done.6) | copy-start | bytes 990724
  231.6 5.0 %collective-permute-start.16 = (f32[2,256]{1,0:T(2,128)S(1)}, f32[2,256]{1,0:T(2,128)S(1)}, u32[]{:S(2)}, u32[]{:S(2)}) collective-permute-start(f32[2,256]{1,0:T(2,128)S(1)} %get-tuple-element.244), channel_id=1, source_target_pairs={{0,8},{8,16},{16,24},{1,9},{9,17},{17,25},{2,10},{10,18},{18,26},{... | collective-permute-start | bytes 6152 | tf_op jit(solution)/shard_map/ppermute | solution.py:31
  235.3 5.5 %collective-permute-start.17 = (f32[2,256]{1,0:T(2,128)S(1)}, f32[2,256]{1,0:T(2,128)S(1)}, u32[]{:S(2)}, u32[]{:S(2)}) collective-permute-start(f32[2,256]{1,0:T(2,128)S(1)} %get-tuple-element.245), channel_id=1, source_target_pairs={{8,0},{16,8},{24,16},{9,1},{17,9},{25,17},{10,2},{18,10},{26,18},{... | collective-permute-start | bytes 6152 | tf_op jit(solution)/shard_map/ppermute | solution.py:34
  236.6 12.0 %copy-start.62 = (f32[2,256]{1,0:T(2,128)}, f32[2,256]{1,0:T(2,128)S(1)}, u32[]{:S(2)}) copy-start(f32[2,256]{1,0:T(2,128)S(1)} %collective-permute-done.16) | copy-start | bytes 6148
  240.7 7.9 %copy-start.63 = (f32[2,256]{1,0:T(2,128)}, f32[2,256]{1,0:T(2,128)S(1)}, u32[]{:S(2)}) copy-start(f32[2,256]{1,0:T(2,128)S(1)} %collective-permute-done.17) | copy-start | bytes 6148
  240.8 2.8 collective-permute-start.18
  242.1 5.6 %collective-permute-start.19 = (f32[12,2]{1,0:T(8,128)S(1)}, f32[12,2]{1,0:T(8,128)S(1)}, u32[]{:S(2)}, u32[]{:S(2)}) collective-permute-start(f32[12,2]{1,0:T(8,128)S(1)} %get-tuple-element.236), channel_id=1, source_target_pairs={{1,0},{2,1},{3,2},{4,3},{5,4},{6,5},{7,6},{9,8},{10,9},{11,10},{12... | collective-permute-start | bytes 296 | tf_op jit(solution)/shard_map/ppermute | solution.py:34
  250.5 8.8 %copy-start.11 = (f32[32,10,258]{2,1,0:T(8,128)S(1)}, f32[32,10,258]{2,1,0:T(8,128)}, u32[]{:S(2)}) copy-start(f32[32,10,258]{2,1,0:T(8,128)} %copy-done.9) | copy-start | bytes 990724
  (37 other events, 67.8 us)
where the time goes:
time: 330 us; the launch traced here: 328 us
  blocking collectives  125 us (38%)
  other arithmetic  112 us (34%)
  starting transfers between devices  54.2 us (16%)
  waiting for transfers between devices  18.6 us (6%)
  local copies, waits for them, and re-layouts  12.1 us (4%)
  between operations  6.23 us (2%)
    psum x2, blocking collectives, residual_dot(): return lax.psum(jnp.sum(residual * precond), ('gx', 'gy'))  82.2 us
    another operation x12, other arithmetic, couple(): return jnp.stack([along_one, along_two])  80.2 us
    psum x1, blocking collectives, on_device(): lax.psum(jnp.sum(direction * image_vec), ('gx', 'gy'))  42.3 us
    ppermute x10, starting transfers between devices, extended(): lax.ppermute(lax.slice_in_dim(block, block.shape[dim] - width, None, axis...  40.8 us
    ppermute x10, waiting for transfers between devices, extended(): lax.ppermute(lax.slice_in_dim(block, 0, width, axis=dim), axis, backward)  18.6 us
    ppermute x10, starting transfers between devices, extended(): lax.ppermute(lax.slice_in_dim(block, 0, width, axis=dim), axis, backward)  13.3 us
  transfers between devices with their start and end apart: 20, of which 6 were waited for; matrix products, arithmetic and copies ran while one was open for 2% of the time, Pallas kernels for 0%

commit v1 on v0

v1 whole, which is shorter than its diff:
```python
import functools

import jax
import jax.numpy as jnp
from jax import lax
from jax.experimental import pallas as pl
from jax.experimental.pallas import tpu as pltpu
from jax.sharding import PartitionSpec as P

vert_coupling = 128.0
sink_rate = 0.0625
bed_drag = 0.5
offset_weight = 0.0019
cross_share = 0.5
reg_gamma = 0.02
reg_smooth = 1.0
diag_scale = 0.003

MESH = pl.DeviceIdType.MESH
REACH = 6
DIRS = [(-1, 0), (1, 0), (0, -1), (0, 1), (-1, -1), (-1, 1), (1, -1), (1, 1)]
OPPOSITE = [1, 0, 3, 2, 7, 6, 5, 4]
FIELDS = 7


def roll(x, shift, axis):
    size = x.shape[axis]
    if isinstance(shift, int):
        shift = shift % size
        if shift == 0:
            return x
    return pltpu.roll(x, shift, axis)


def near(x, step, axis):
    return roll(x, -step, axis)


def kernel(
    nx, ny,
    grad_ref, warm_ref, visc_ref, fric_ref, slide_ref, obs_ref, ice_ref, ground_ref,
    sol_ref, res_ref,
    up, down, bot, gbot, top, gtop,
    row_send, row_recv, f_send, f_recv, p_send, p_recv, k_send, k_recv, kp_send, kp_recv,
    ext, red, slots,
    s_send, s_recv, r_send, r_recv,
):
    levels, rows, cols = visc_ref.shape
    n = nx * ny
    ix, iy = lax.axis_index("gx"), lax.axis_index("gy")
    me = ix * ny + iy

    barrier = pltpu.get_barrier_semaphore()

    def greet(j, c):
        peer = lax.rem(me + j, n)
        pl.semaphore_signal(barrier, inc=1, device_id=(peer // ny, lax.rem(peer, ny)), device_id_type=MESH)
        return c

    lax.fori_loop(1, n, greet, 0)

    def exists(d):
        dx, dy = DIRS[d]
        x, y = ix + dx, iy + dy
        return (x >= 0) & (x < nx) & (y >= 0) & (y < ny)

    def copy(src, dst, d, sem):
        dx, dy = DIRS[d]
        return pltpu.make_async_remote_copy(
            src_ref=src, dst_ref=dst,
            send_sem=s_send.at[sem + d], recv_sem=s_recv.at[sem + OPPOSITE[d]],
            device_id=(jnp.clip(ix + dx, 0, nx - 1), jnp.clip(iy + dy, 0, ny - 1)),
            device_id_type=MESH,
        )

    def messages(d, stage):
        o = OPPOSITE[d]
        side = 0 if DIRS[d][1] < 0 else 1
        if stage == 0:
            if d < 2:
                return [copy(row_send.at[d], row_recv.at[o], d, 0), copy(f_send, f_recv.at[o], d, 8)]
            return [copy(p_send.at[side], p_recv.at[o - 2], d, 0)]
        if d < 2:
            return [copy(k_send, k_recv.at[o], d, 16)]
        return [copy(kp_send.at[side], kp_recv.at[o - 2], d, 16)]

    def clear(d, stage):
        if stage == 0:
            refs = [row_recv.at[d], f_recv.at[d]] if d < 2 else [p_recv.at[d - 2]]
        else:
            refs = [k_recv.at[d]] if d < 2 else [kp_recv.at[d - 2]]
        for ref in refs:
            ref[...] = jnp.zeros(ref.shape, jnp.float32)

    def start(stage):
        for d in range(8):
            @pl.when(exists(d))
            def _():
                for m in messages(d, stage):
                    m.start()

    def finish_recv(stage):
        for d in range(8):
            @pl.when(exists(d))
            def _():
                o = OPPOSITE[d]
                for m in messages(o, stage):
                    m.wait_recv()

    def finish_send(stage):
        for d in range(8):
            @pl.when(exists(d))
            def _():
                for m in messages(d, stage):
                    m.wait_send()

    for stage in (0, 1):
        for d in range(8):
            @pl.when(jnp.logical_not(exists(d)))
            def _():
                clear(d, stage)

    ice = ice_ref[...].astype(jnp.float32)
    ground = ground_ref[...].astype(jnp.float32)
    fric = fric_ref[...]
    friction = ground * fric
    base = ice * ground * fric
    inverse = 1.0 / (reg_gamma * (1.0 + 4.0 * reg_smooth) + diag_scale * base * fric)
    lane = lax.broadcasted_iota(jnp.int32, (rows, 128), 1)

    def eliminate(i, carry):
        e, f = carry
        k = levels - 2 - i
        v_low, v_up = visc_ref[i], visc_ref[i + 1]
        link = (vert_coupling * 0.5) * (v_low + v_up)
        ratio = link / (link + e)
        up[i] = ratio
        e = sink_rate * v_up + e * ratio
        w_low, w_up = visc_ref[k], visc_ref[k + 1]
        link = (vert_coupling * 0.5) * (w_low + w_up)
        ratio = link / (link + f)
        down[k] = ratio
        f = sink_rate * w_low + f * ratio
        return e, f

    e = sink_rate * visc_ref[0] + bed_drag * friction
    f = sink_rate * visc_ref[levels - 1]
    e, f = lax.fori_loop(0, levels - 1, eliminate, (e, f))

    zero = jnp.zeros((rows, cols), jnp.float32)
    for ref in (top, gtop):
        ref[0] = zero
        ref[levels + 1] = zero

    def respond(z, carry):
        b, t, left, right = carry
        g = visc_ref[z] * b
        bot[z] = b
        gbot[z] = g
        for j, val in ((0, b), (levels, g)):
            row_send[0, pl.ds(z + j, 1), :] = val[:1]
            row_send[1, pl.ds(z + j, 1), :] = val[rows - 1:]
            left = jnp.where(lane == z + j, roll(val[:, :128], z + j, 1), left)
            right = jnp.where(lane == z + j, roll(val[:, cols - 128:], z + j + 1, 1), right)
        k = levels - 1 - z
        top[k + 1] = t
        gtop[k + 1] = visc_ref[k] * t
        t = t * up[jnp.maximum(k - 1, 0)]
        b = b * down[jnp.minimum(z, levels - 2)]
        return b, t, left, right

    blank = jnp.zeros((rows, 128), jnp.float32)
    _, _, left, right = lax.fori_loop(
        0, levels, respond, (1.0 / (f + bed_drag * friction), 1.0 / e, blank, blank)
    )

    own = [base * slide_ref[0], base * slide_ref[1], ice * obs_ref[...], inverse, bot[levels - 1], warm_ref[...], grad_ref[...]]

    def pack(fields, place, left, right):
        for val in fields:
            here = (lane >= place) & (lane < place + REACH)
            left = jnp.where(here, roll(val[:, :128], place, 1), left)
            right = jnp.where(here, roll(val[:, cols - 128:], place - (128 - REACH), 1), right)
            place += REACH
        return left, right

    left, right = pack(own, 2 * levels, left, right)
    for j, val in enumerate(own):
        f_send[j] = val
    p_send[0] = left
    p_send[1] = right

    pl.semaphore_wait(barrier, n - 1)
    start(0)
    finish_recv(0)

    row_id = lax.broadcasted_iota(jnp.int32, (rows, cols), 0)
    col_id = lax.broadcasted_iota(jnp.int32, (rows, cols), 1)
    prow = lax.broadcasted_iota(jnp.int32, (rows, 128), 0)

    def beside(side):
        at = {dx: p_recv[DIRS.index((dx, side)) - 2] for dx in (-1, 0, 1)}
        return {
            -1: jnp.where(prow == 0, near(at[-1], -1, 0), near(at[0], -1, 0)),
            0: at[0],
            1: jnp.where(prow == rows - 1, near(at[1], 1, 0), near(at[0], 1, 0)),
        }

    packs = {side: beside(side) for side in (-1, 1)}

    def gather(z, acc):
        acc = list(acc)
        weights = []
        for ref in (gtop, top):
            mid, out = ref[z + 1], ref[z] + ref[z + 2]
            weights.append((
                (0.5 * offset_weight) * mid + (0.25 * offset_weight) * out,
                (0.25 * offset_weight) * mid + (0.5 * offset_weight / 3.0) * out,
            ))
        for j, ref, weight in ((0, bot, weights[0]), (levels, gbot, weights[1])):
            mid = ref[z]
            low = jnp.where(row_id == 0, row_recv[0, pl.ds(z + j, 1), :], near(mid, -1, 0))
            high = jnp.where(row_id == rows - 1, row_recv[1, pl.ds(z + j, 1), :], near(mid, 1, 0))
            for dx, val in ((-1, low), (0, mid), (1, high)):
                from_left = roll(packs[-1][dx], lax.rem(128 - z - j, 128), 1)
                from_right = roll(packs[1][dx], 127 - z - j, 1)
                wide = lambda x: jnp.concatenate([x] * (cols // 128), axis=1)
                sides = {
                    -1: jnp.where(col_id == 0, wide(from_left), near(val, -1, 1)),
                    0: val,
                    1: jnp.where(col_id == cols - 1, wide(from_right), near(val, 1, 1)),
                }
                for dy in (-1, 0, 1):
                    if (dx, dy) != (0, 0):
                        d = DIRS.index((dx, dy))
                        acc[d] = acc[d] + weight[1 if dx * dy != 0 else 0] * sides[dy]
        return tuple(acc)

    coefs = lax.fori_loop(0, levels, gather, (zero,) * 8)
    for d in range(8):
        k_send[d] = coefs[d]
    kleft, kright = pack(coefs, 0, blank, blank)
    kp_send[0] = kleft
    kp_send[1] = kright
    start(1)

    def extend(j, mine, recv, packs_ref, index, place):
        for tile, dx in enumerate((-1, 0, 1)):
            here = mine if dx == 0 else recv[0 if dx < 0 else 1, index]
            from_right = packs_ref[DIRS.index((dx, 1)) - 2]
            from_left = packs_ref[DIRS.index((dx, -1)) - 2]
            halo = jnp.where(lane < REACH, roll(from_right, -place, 1), 0.0)
            halo = jnp.where(lane >= 128 - REACH, roll(from_left, 128 - REACH - place, 1), halo)
            ext[j, tile * rows:(tile + 1) * rows, :cols] = here
            ext[j, tile * rows:(tile + 1) * rows, cols:] = halo

    for j in range(FIELDS):
        extend(j, f_send[j], f_recv, p_recv, j, 2 * levels + REACH * j)
    finish_recv(1)
    for d in range(8):
        extend(FIELDS + d, k_send[d], k_recv, kp_recv, d, REACH * d)

    def coef(dx, dy):
        return ext[FIELDS + DIRS.index((dx, dy))]

    def hessian(q):
        spread = [ext[0] * q, ext[1] * q]
        surface = [ext[4] * spread[0], ext[4] * spread[1]]
        for dx in (-1, 0, 1):
            moved = [near(s, dx, 0) for s in spread]
            for dy in (-1, 0, 1):
                if (dx, dy) == (0, 0):
                    continue
                share = cross_share * dx * dy
                for c in range(2):
                    val = moved[c] if share == 0 else moved[c] + share * moved[1 - c]
                    surface[c] = surface[c] + coef(dx, dy) * near(val, dy, 1)
        traction = [ext[2] * s for s in surface]
        basal = [ext[4] * t for t in traction]
        for dx in (-1, 0, 1):
            part = [None, None]
            for dy in (-1, 0, 1):
                if (dx, dy) == (0, 0):
                    continue
                share = cross_share * dx * dy
                for c in range(2):
                    val = traction[c] if share == 0 else traction[c] + share * traction[1 - c]
                    val = near(coef(-dx, -dy) * val, dy, 1)
                    part[c] = val if part[c] is None else part[c] + val
            basal = [basal[c] + near(part[c], dx, 0) for c in range(2)]
        around = near(q, 1, 0) + near(q, -1, 0) + near(q, 1, 1) + near(q, -1, 1)
        smooth = reg_gamma * (q + reg_smooth * (4.0 * q - around))
        return ext[0] * basal[0] + ext[1] * basal[1] + smooth

    def mine(x):
        return x[rows:2 * rows, :cols]

    warm = ext[5]
    r0 = ext[6] - hessian(warm)
    p0 = ext[3] * r0
    w0 = hessian(p0)
    y0 = ext[3] * w0
    u0 = mine(hessian(y0))
    r0, p0, w0, y0 = mine(r0), mine(p0), mine(w0), mine(y0)

    def total(x):
        return jnp.sum(jnp.sum(x, axis=0, keepdims=True), axis=1, keepdims=True)

    one_lane = lax.broadcasted_iota(jnp.int32, (1, 128), 1)
    sums = jnp.zeros((1, 128), jnp.float32)
    for j, val in enumerate((r0 * p0, p0 * w0, w0 * y0, y0 * u0)):
        sums = jnp.where(one_lane == j, total(val), sums)
    red[...] = sums

    def to_peer(j, index):
        peer = lax.rem(me + j, n)
        return pltpu.make_async_remote_copy(
            src_ref=red, dst_ref=slots.at[index],
            send_sem=r_send.at[j], recv_sem=r_recv.at[index],
            device_id=(peer // ny, lax.rem(peer, ny)), device_id_type=MESH,
        )

    def send(j, c):
        to_peer(j, me).start()
        return c

    def receive(j, c):
        to_peer(j, lax.rem(me + j, n)).wait_recv()
        return c

    def sent(j, c):
        to_peer(j, me).wait_send()
        return c

    lax.fori_loop(1, n, send, 0)
    lax.fori_loop(1, n, receive, 0)
    slots[me] = sums
    everyone = jnp.sum(slots[...], axis=0)

    def pick(j):
        return jnp.sum(jnp.where(one_lane == j, everyone, 0.0), axis=1, keepdims=True)

    rz0, pw, wy, yu = pick(0), pick(1), pick(2), pick(3)
    a0 = rz0 / pw
    rz1 = a0 * a0 * wy - rz0
    beta = rz1 / rz0
    more = 1.0 + beta
    curve = more * (more * pw - 2.0 * a0 * wy) + a0 * a0 * yu
    a1 = rz1 / curve
    sol_ref[...] = warm_ref[...] + a0 * p0 + a1 * (more * p0 - a0 * y0)
    res_ref[...] = r0 - a0 * w0 - a1 * (more * w0 - a0 * u0)

    finish_send(0)
    finish_send(1)
    lax.fori_loop(1, n, sent, 0)


def solution(mesh):
    nx, ny = mesh.shape["gx"], mesh.shape["gy"]
    n = nx * ny

    def on_device(gradient, warm_start, viscosity, friction_coef, slide_dir, obs_weight, ice_mask, grounded):
        levels, rows, cols = viscosity.shape
        vmem = pl.BlockSpec(memory_space=pltpu.VMEM)
        f32 = lambda *shape: pltpu.VMEM(shape, jnp.float32)
        return tuple(pl.pallas_call(
            functools.partial(kernel, nx, ny),
            out_shape=[jax.ShapeDtypeStruct((rows, cols), jnp.float32)] * 2,
            in_specs=[vmem] * 8,
            out_specs=[vmem] * 2,
            scratch_shapes=[
                f32(levels, rows, cols), f32(levels, rows, cols),
                f32(levels, rows, cols), f32(levels, rows, cols),
                f32(levels + 2, rows, cols), f32(levels + 2, rows, cols),
                f32(2, 2 * levels, cols), f32(2, 2 * levels, cols),
                f32(FIELDS, rows, cols), f32(2, FIELDS, rows, cols),
                f32(2, rows, 128), f32(6, rows, 128),
                f32(8, rows, cols), f32(2, 8, rows, cols),
                f32(2, rows, 128), f32(6, rows, 128),
                f32(FIELDS + 8, 3 * rows, cols + 128),
                f32(1, 128), f32(n, 1, 128),
                pltpu.SemaphoreType.DMA((24,)), pltpu.SemaphoreType.DMA((24,)),
                pltpu.SemaphoreType.DMA((n,)), pltpu.SemaphoreType.DMA((n,)),
            ],
            compiler_params=pltpu.CompilerParams(collective_id=0, has_side_effects=True),
        )(gradient, warm_start, viscosity, friction_coef, slide_dir, obs_weight, ice_mask, grounded))

    flat = P("gx", "gy")
    deep = P(None, "gx", "gy")
    return jax.shard_map(
        on_device,
        mesh=mesh,
        in_specs=(flat, flat, deep, flat, deep, flat, flat, flat),
        out_specs=(flat, flat),
        check_vma=False,
    )
```

time: 330 us -> 31.1 us (0.09)
  blocking collectives: 125 us -> 0 us
  other arithmetic: 112 us -> 0 us
  starting transfers between devices: 54.2 us -> 0 us
  Pallas kernels: 0 us -> 28.4 us
  waiting for transfers between devices: 18.6 us -> 0 us
  local copies, waits for them, and re-layouts: 12.1 us -> 1.9 us
  between operations: 6.23 us -> 0.65 us
    psum x3 -> x0, blocking collectives: 125 us -> none  [the longest x2 82.2 us: residual_dot(): return lax.psum(jnp.sum(residual * precond), ('gx', 'gy'))]
    another operation x13 -> x0, other arithmetic: 80.2 us -> none  [the longest x12 80.2 us: couple(): return jnp.stack([along_one, along_two])]
    ppermute x20 -> x0, starting transfers between devices: 54.2 us -> none  [the longest x10 40.8 us: extended(): lax.ppermute(lax.slice_in_dim(block, block.shape[dim] - width, None, axis...]
    pallas_call x0 -> x1, Pallas kernels: none -> 28.4 us  [on_device(): pl.pallas_call(functools.partial(kernel, nx, ny), out_shape=[jax.ShapeDty...]
    ppermute x20 -> x0, waiting for transfers between devices: 18.6 us -> none  [the longest x10 18.6 us: extended(): lax.ppermute(lax.slice_in_dim(block, 0, width, axis=dim), axis, backward)]
    reduce_sum x12 -> x0, other arithmetic: 16.1 us -> none  [the longest x3 4.79 us: hessian(): jnp.sum(top_inner[None] * coupled, axis=1)]
    mul x33 -> x0, other arithmetic: 8.43 us -> none  [the longest x3 2.58 us: hessian(): first_state = bottom_wide[None] * spread[:, None]]
    slice x12 -> x0, local copies, waits for them, and re-layouts: 4.63 us -> none  [the longest x9 2.29 us: extended(): lax.slice_in_dim(block, block.shape[dim] - width, None, axis=dim)]
  transfers between devices with their start and end apart: 20 -> 0, of which waited for: 6 -> 0; matrix products, arithmetic and copies ran while one was open for 2% -> 0% of each run, Pallas kernels for 0% -> 0%
where the time goes in v1:
time: 31.1 us; the launch traced here: 30.9 us
  Pallas kernels  28.4 us (91%)
  local copies, waits for them, and re-layouts  1.9 us (6%)
  between operations  0.65 us (2%)
    pallas_call x1, Pallas kernels, on_device(): pl.pallas_call(functools.partial(kernel, nx, ny), out_shape=[jax.ShapeDty...  28.4 us
    unnamed x4, local copies, waits for them, and re-layouts  1.9 us

profile of v1, /device:TPU:0, one launch (start us, length us, event | category | flops | bytes accessed | tf_op | source)
XLA Modules:
  0.0 30.9 jit_solution(1074311133143531682)
XLA Ops:
  0.6 28.4 %shard_map.95 = (f32[8,256]{1,0:T(8,128)}, f32[8,256]{1,0:T(8,128)}) custom-call(f32[8,256]{1,0:T(8,128)} %grad_ref.1, f32[8,256]{1,0:T(8,128)} %warm_ref.1, f32[32,8,256]{2,1,0:T(8,128)} %visc_ref.1, f32[8,256]{1,0:T(8,128)} %fric_ref.1, f32[2,8,256]{2,1,0:T(8,128)} %slide_ref.1, f32[8,256]{1,0:T(8,128)} %obs_ref.1, s32[8,256]{1,0:T(8,128)} %ice_ref.1, ...), custom_call_target="tpu_custom_call" | custom-call | tf_op jit(solution)/shard_map/pallas_call | solution.py:366
  29.0 0.0 copy-start
  29.0 1.3 %copy.12 = f32[8,256]{1,0:T(8,128)} copy(f32[8,256]{1,0:T(8,128)} %get-tuple-element.4) | data formatting | bytes 16384
  30.3 0.0 copy-done
  30.3 0.6 %copy.13 = f32[8,256]{1,0:T(8,128)} copy(f32[8,256]{1,0:T(8,128)S(1)} %copy-done) | data formatting | bytes 16384
Async XLA Ops:
  29.0 1.3 %copy-start = (f32[8,256]{1,0:T(8,128)S(1)}, f32[8,256]{1,0:T(8,128)}, u32[]{:S(2)}) copy-start(f32[8,256]{1,0:T(8,128)} %get-tuple-element.5) | copy-start | bytes 24580

commit v2 on v1

--- a/solution.py
+++ b/solution.py
@@ -38,31 +38,50 @@
 
 def kernel(
     nx, ny,
+    grad_in, warm_in, visc_in, fric_in, slide_in, obs_in, ice_in, ground_in,
+    out_ref,
     grad_ref, warm_ref, visc_ref, fric_ref, slide_ref, obs_ref, ice_ref, ground_ref,
-    sol_ref, res_ref,
     up, down, bot, gbot, top, gtop,
     row_send, row_recv, f_send, f_recv, p_send, p_recv, k_send, k_recv, kp_send, kp_recv,
     ext, red, slots,
-    s_send, s_recv, r_send, r_recv,
+    load_sem, s_send, s_recv, r_send, r_recv, all_in,
 ):
     levels, rows, cols = visc_ref.shape
     n = nx * ny
     ix, iy = lax.axis_index("gx"), lax.axis_index("gy")
     me = ix * ny + iy
 
-    barrier = pltpu.get_barrier_semaphore()
-
-    def greet(j, c):
-        peer = lax.rem(me + j, n)
-        pl.semaphore_signal(barrier, inc=1, device_id=(peer // ny, lax.rem(peer, ny)), device_id_type=MESH)
-        return c
-
-    lax.fori_loop(1, n, greet, 0)
+    loads = [
+        pltpu.make_async_copy(src, dst, load_sem.at[j])
+        for j, (src, dst) in enumerate((
+            (visc_in, visc_ref), (fric_in, fric_ref), (ground_in, ground_ref), (ice_in, ice_ref),
+            (slide_in, slide_ref), (obs_in, obs_ref), (warm_in, warm_ref), (grad_in, grad_ref),
+        ))
+    ]
 
     def exists(d):
         dx, dy = DIRS[d]
         x, y = ix + dx, iy + dy
         return (x >= 0) & (x < nx) & (y >= 0) & (y < ny)
+
+    barrier = pltpu.get_barrier_semaphore()
+
+    def greet(x, y):
+        pl.semaphore_signal(barrier, inc=1, device_id=(x, y), device_id_type=MESH)
+
+    for load in loads:
+        load.start()
+    expected = nx - 1 + ny - 1
+    for d in range(4, 8):
+        expected = expected + exists(d).astype(jnp.int32)
+
+        @pl.when(exists(d))
+        def _():
+            greet(ix + DIRS[d][0], iy + DIRS[d][1])
+    for k in range(1, nx):
+        greet(lax.rem(ix + k, nx), iy)
+    for k in range(1, ny):
+        greet(ix, lax.rem(iy + k, ny))
 
     def copy(src, dst, d, sem):
         dx, dy = DIRS[d]
@@ -73,52 +92,45 @@
             device_id_type=MESH,
         )
 
-    def messages(d, stage):
+    def message(d, what):
         o = OPPOSITE[d]
         side = 0 if DIRS[d][1] < 0 else 1
-        if stage == 0:
-            if d < 2:
-                return [copy(row_send.at[d], row_recv.at[o], d, 0), copy(f_send, f_recv.at[o], d, 8)]
-            return [copy(p_send.at[side], p_recv.at[o - 2], d, 0)]
-        if d < 2:
-            return [copy(k_send, k_recv.at[o], d, 16)]
-        return [copy(kp_send.at[side], kp_recv.at[o - 2], d, 16)]
-
-    def clear(d, stage):
-        if stage == 0:
-            refs = [row_recv.at[d], f_recv.at[d]] if d < 2 else [p_recv.at[d - 2]]
-        else:
-            refs = [k_recv.at[d]] if d < 2 else [kp_recv.at[d - 2]]
-        for ref in refs:
-            ref[...] = jnp.zeros(ref.shape, jnp.float32)
-
-    def start(stage):
-        for d in range(8):
-            @pl.when(exists(d))
-            def _():
-                for m in messages(d, stage):
-                    m.start()
-
-    def finish_recv(stage):
-        for d in range(8):
-            @pl.when(exists(d))
-            def _():
-                o = OPPOSITE[d]
-                for m in messages(o, stage):
-                    m.wait_recv()
-
-    def finish_send(stage):
-        for d in range(8):
-            @pl.when(exists(d))
-            def _():
-                for m in messages(d, stage):
-                    m.wait_send()
-
-    for stage in (0, 1):
-        for d in range(8):
-            @pl.when(jnp.logical_not(exists(d)))
-            def _():
-                clear(d, stage)
+        return {
+            "row": lambda: copy(row_send.at[d], row_recv.at[o], d, 0),
+            "field": lambda: copy(f_send, f_recv.at[o], d, 8),
+            "coef": lambda: copy(k_send, k_recv.at[o], d, 16),
+            "pack": lambda: copy(p_send.at[side], p_recv.at[o - 2], d, 0),
+            "coefpack": lambda: copy(kp_send.at[side], kp_recv.at[o - 2], d, 16),
+        }[what]()
+
+    beside_x, others = (0, 1), range(2, 8)
+    kinds = (("row", beside_x), ("pack", others), ("field", beside_x), ("coefpack", others), ("coef", beside_x))
+
+    def each(action, names):
+        for name, towards in kinds:
+            if name not in names:
+                continue
+            for d in towards:
+                @pl.when(exists(d))
+                def _():
+                    if action == "wait_recv":
+                        message(OPPOSITE[d], name).wait_recv()
+                    elif action == "wait_send":
+                        message(d, name).wait_send()
+                    else:
+                        message(d, name).start()
+
+    def clear(ref):
+        ref[...] = jnp.zeros(ref.shape, jnp.float32)
+
+    for d in range(8):
+        @pl.when(jnp.logical_not(exists(d)))
+        def _():
+            for ref in (row_recv, f_recv, k_recv) if d < 2 else (p_recv, kp_recv):
+                clear(ref.at[d if d < 2 else d - 2])
+
+    for load in loads:
+        load.wait()
 
     ice = ice_ref[...].astype(jnp.float32)
     ground = ground_ref[...].astype(jnp.float32)
@@ -145,7 +157,7 @@
 
     e = sink_rate * visc_ref[0] + bed_drag * friction
     f = sink_rate * visc_ref[levels - 1]
-    e, f = lax.fori_loop(0, levels - 1, eliminate, (e, f))
+    e, f = lax.fori_loop(0, levels - 1, eliminate, (e, f), unroll=True)
 
     zero = jnp.zeros((rows, cols), jnp.float32)
     for ref in (top, gtop):
@@ -171,7 +183,7 @@
 
     blank = jnp.zeros((rows, 128), jnp.float32)
     _, _, left, right = lax.fori_loop(
-        0, levels, respond, (1.0 / (f + bed_drag * friction), 1.0 / e, blank, blank)
+        0, levels, respond, (1.0 / (f + bed_drag * friction), 1.0 / e, blank, blank), unroll=4
     )
 
     own = [base * slide_ref[0], base * slide_ref[1], ice * obs_ref[...], inverse, bot[levels - 1], warm_ref[...], grad_ref[...]]
@@ -190,9 +202,11 @@
     p_send[0] = left
     p_send[1] = right
 
-    pl.semaphore_wait(barrier, n - 1)
-    start(0)
-    finish_recv(0)
+    pl.semaphore_wait(barrier, expected)
+    each("start", ("row", "pack", "field"))
+    for k in range(1, ny):
+        pl.semaphore_signal(all_in, inc=1, device_id=(ix, lax.rem(iy + k, ny)), device_id_type=MESH)
+    each("wait_recv", ("row", "pack"))
 
     row_id = lax.broadcasted_iota(jnp.int32, (rows, cols), 0)
     col_id = lax.broadcasted_iota(jnp.int32, (rows, cols), 1)
@@ -236,13 +250,13 @@
                         acc[d] = acc[d] + weight[1 if dx * dy != 0 else 0] * sides[dy]
         return tuple(acc)
 
-    coefs = lax.fori_loop(0, levels, gather, (zero,) * 8)
+    coefs = lax.fori_loop(0, levels, gather, (zero,) * 8, unroll=4)
     for d in range(8):
         k_send[d] = coefs[d]
     kleft, kright = pack(coefs, 0, blank, blank)
     kp_send[0] = kleft
     kp_send[1] = kright
-    start(1)
+    each("start", ("coefpack", "coef"))
 
     def extend(j, mine, recv, packs_ref, index, place):
         for tile, dx in enumerate((-1, 0, 1)):
@@ -254,16 +268,17 @@
             ext[j, tile * rows:(tile + 1) * rows, :cols] = here
             ext[j, tile * rows:(tile + 1) * rows, cols:] = halo
 
+    each("wait_recv", ("field",))
     for j in range(FIELDS):
         extend(j, f_send[j], f_recv, p_recv, j, 2 * levels + REACH * j)
-    finish_recv(1)
+    each("wait_recv", ("coefpack", "coef"))
     for d in range(8):
         extend(FIELDS + d, k_send[d], k_recv, kp_recv, d, REACH * d)
 
     def coef(dx, dy):
         return ext[FIELDS + DIRS.index((dx, dy))]
 
-    def hessian(q):
+    def forth(q):
         spread = [ext[0] * q, ext[1] * q]
         surface = [ext[4] * spread[0], ext[4] * spread[1]]
         for dx in (-1, 0, 1):
@@ -275,6 +290,9 @@
                 for c in range(2):
                     val = moved[c] if share == 0 else moved[c] + share * moved[1 - c]
                     surface[c] = surface[c] + coef(dx, dy) * near(val, dy, 1)
+        return surface
+
+    def back(q, surface):
         traction = [ext[2] * s for s in surface]
         basal = [ext[4] * t for t in traction]
         for dx in (-1, 0, 1):
@@ -288,19 +306,27 @@
                     val = near(coef(-dx, -dy) * val, dy, 1)
                     part[c] = val if part[c] is None else part[c] + val
             basal = [basal[c] + near(part[c], dx, 0) for c in range(2)]
+        return ext[0] * basal[0] + ext[1] * basal[1] + regularize(q)
+
+    def regularize(q):
         around = near(q, 1, 0) + near(q, -1, 0) + near(q, 1, 1) + near(q, -1, 1)
-        smooth = reg_gamma * (q + reg_smooth * (4.0 * q - around))
-        return ext[0] * basal[0] + ext[1] * basal[1] + smooth
+        return reg_gamma * (q + reg_smooth * (4.0 * q - around))
+
+    def hessian(q):
+        return back(q, forth(q))
 
     def mine(x):
         return x[rows:2 * rows, :cols]
 
     warm = ext[5]
-    r0 = ext[6] - hessian(warm)
+    image = hessian(warm)
+    r0 = ext[6] - image
     p0 = ext[3] * r0
     w0 = hessian(p0)
     y0 = ext[3] * w0
-    u0 = mine(hessian(y0))
+    surface = forth(y0)
+    curve0 = mine(ext[2]) * (mine(surface[0]) * mine(surface[0]) + mine(surface[1]) * mine(surface[1])) + mine(y0 * regularize(y0))
+    full_y0 = y0
     r0, p0, w0, y0 = mine(r0), mine(p0), mine(w0), mine(y0)
 
     def total(x):
@@ -308,7 +334,7 @@
 
     one_lane = lax.broadcasted_iota(jnp.int32, (1, 128), 1)
     sums = jnp.zeros((1, 128), jnp.float32)
-    for j, val in enumerate((r0 * p0, p0 * w0, w0 * y0, y0 * u0)):
+    for j, val in enumerate((r0 * p0, p0 * w0, w0 * y0, curve0)):
         sums = jnp.where(one_lane == j, total(val), sums)
     red[...] = sums
 
@@ -332,8 +358,11 @@
         to_peer(j, me).wait_send()
         return c
 
-    lax.fori_loop(1, n, send, 0)
-    lax.fori_loop(1, n, receive, 0)
+    pl.semaphore_wait(all_in, ny - 1)
+    lax.fori_loop(1, n, send, 0, unroll=4)
+    u0 = mine(back(full_y0, surface))
+    each("wait_send", [name for name, _ in kinds])
+    lax.fori_loop(1, n, receive, 0, unroll=4)
     slots[me] = sums
     everyone = jnp.sum(slots[...], axis=0)
 
@@ -347,11 +376,8 @@
     more = 1.0 + beta
     curve = more * (more * pw - 2.0 * a0 * wy) + a0 * a0 * yu
     a1 = rz1 / curve
-    sol_ref[...] = warm_ref[...] + a0 * p0 + a1 * (more * p0 - a0 * y0)
-    res_ref[...] = r0 - a0 * w0 - a1 * (more * w0 - a0 * u0)
-
-    finish_send(0)
-    finish_send(1)
+    out_ref[0] = a0 * p0 + a1 * (more * p0 - a0 * y0)
+    out_ref[1] = -mine(image) - a0 * w0 - a1 * (more * w0 - a0 * u0)
     lax.fori_loop(1, n, sent, 0)
 
 
@@ -363,12 +389,14 @@
         levels, rows, cols = viscosity.shape
         vmem = pl.BlockSpec(memory_space=pltpu.VMEM)
         f32 = lambda *shape: pltpu.VMEM(shape, jnp.float32)
-        return tuple(pl.pallas_call(
+        flat = (gradient, warm_start, viscosity, friction_coef, slide_dir, obs_weight, ice_mask, grounded)
+        change = pl.pallas_call(
             functools.partial(kernel, nx, ny),
-            out_shape=[jax.ShapeDtypeStruct((rows, cols), jnp.float32)] * 2,
-            in_specs=[vmem] * 8,
-            out_specs=[vmem] * 2,
+            out_shape=jax.ShapeDtypeStruct((2, rows, cols), jnp.float32),
+            in_specs=[pl.BlockSpec(memory_space=pl.ANY)] * 8,
+            out_specs=vmem,
             scratch_shapes=[
+                *(pltpu.VMEM(a.shape, a.dtype) for a in flat),
                 f32(levels, rows, cols), f32(levels, rows, cols),
                 f32(levels, rows, cols), f32(levels, rows, cols),
                 f32(levels + 2, rows, cols), f32(levels + 2, rows, cols),
@@ -379,11 +407,14 @@
                 f32(2, rows, 128), f32(6, rows, 128),
                 f32(FIELDS + 8, 3 * rows, cols + 128),
                 f32(1, 128), f32(n, 1, 128),
+                pltpu.SemaphoreType.DMA((8,)),
                 pltpu.SemaphoreType.DMA((24,)), pltpu.SemaphoreType.DMA((24,)),
                 pltpu.SemaphoreType.DMA((n,)), pltpu.SemaphoreType.DMA((n,)),
+                pltpu.SemaphoreType.REGULAR,
             ],
             compiler_params=pltpu.CompilerParams(collective_id=0, has_side_effects=True),
-        )(gradient, warm_start, viscosity, friction_coef, slide_dir, obs_weight, ice_mask, grounded))
+        )(*flat)
+        return warm_start + change[0], gradient + change[1]
 
     flat = P("gx", "gy")
     deep = P(None, "gx", "gy")

time: 31.1 us -> 25.2 us (0.81)
  Pallas kernels: 28.4 us -> 23 us
  local copies, waits for them, and re-layouts: 1.9 us -> 0.01 us
  other arithmetic: 0 us -> 1.32 us
    pallas_call x1, Pallas kernels: 28.4 us -> 23 us  [on_device(): pl.pallas_call(functools.partial(kernel, nx, ny), out_shape=jax.ShapeDtyp...]
    unnamed x4, local copies, waits for them, and re-layouts: 1.9 us -> 0.01 us
    add x0 -> x1, other arithmetic: none -> 1.32 us  [on_device(): return (warm_start + change[0], gradient + change[1])]
where the time goes in v2:
time: 25.2 us; the launch traced here: 25 us
  Pallas kernels  23 us (91%)
  other arithmetic  1.32 us (5%)
  between operations  0.67 us (3%)
    pallas_call x1, Pallas kernels, on_device(): pl.pallas_call(functools.partial(kernel, nx, ny), out_shape=jax.ShapeDtyp...  23 us
    add x1, other arithmetic, on_device(): return (warm_start + change[0], gradient + change[1])  1.32 us

profile of v2, /device:TPU:0, one launch (start us, length us, event | category | flops | bytes accessed | tf_op | source)
XLA Modules:
  0.0 25.0 jit_solution(8041049474487211371)
XLA Ops:
  0.6 0.0 copy-start.1
  0.6 0.0 copy-start
  0.7 23.0 %shard_map.95 = f32[2,8,256]{2,1,0:T(8,128)} custom-call(f32[8,256]{1,0:T(8,128)} %grad_in.1, f32[8,256]{1,0:T(8,128)} %warm_in.1, f32[32,8,256]{2,1,0:T(8,128)} %visc_in.1, f32[8,256]{1,0:T(8,128)} %fric_in.1, f32[2,8,256]{2,1,0:T(8,128)} %slide_in.1, f32[8,256]{1,0:T(8,128)} %obs_in.1, s32[8,256]{1,0:T(8,128)} %ice_in.1, s32[8,256]{1,0:T(8,128)} %ground_in.1), custom_call_target="tpu_custom_call" | custom-call | tf_op jit(solution)/shard_map/pallas_call | solution.py:393
  23.7 0.0 copy-done.1
  23.7 0.0 copy-done
  23.7 1.3 %bitcast_add_fusion = (f32[8,256]{1,0:T(8,128)}, f32[8,256]{1,0:T(8,128)}) fusion(f32[8,256]{1,0:T(8,128)S(1)} %copy-done, f32[2,8,256]{2,1,0:T(8,128)} %shard_map.95, f32[8,256]{1,0:T(8,128)S(1)} %copy-done.1), kind=kLoop, calls=%fused_computation | loop fusion | flops 4096 | bytes 49152 | tf_op jit(solution)/shard_map/add | solution.py:417
Async XLA Ops:
  0.6 23.0 %copy-start.1 = (f32[8,256]{1,0:T(8,128)S(1)}, f32[8,256]{1,0:T(8,128)}, u32[]{:S(2)}) copy-start(f32[8,256]{1,0:T(8,128)} %warm_in.1) | copy-start | bytes 24580
  0.6 23.0 %copy-start = (f32[8,256]{1,0:T(8,128)S(1)}, f32[8,256]{1,0:T(8,128)}, u32[]{:S(2)}) copy-start(f32[8,256]{1,0:T(8,128)} %grad_in.1) | copy-start | bytes 24580

commit v3 on v2

--- a/solution.py
+++ b/solution.py
@@ -42,7 +42,7 @@
     out_ref,
     grad_ref, warm_ref, visc_ref, fric_ref, slide_ref, obs_ref, ice_ref, ground_ref,
     up, down, bot, gbot, top, gtop,
-    row_send, row_recv, f_send, f_recv, p_send, p_recv, k_send, k_recv, kp_send, kp_recv,
+    t_row, row_send, row_recv, f_send, f_recv, p_send, p_recv, k_send, k_recv, kp_send, kp_recv,
     ext, red, slots,
     load_sem, s_send, s_recv, r_send, r_recv, all_in,
 ):
@@ -165,7 +165,7 @@
         ref[levels + 1] = zero
 
     def respond(z, carry):
-        b, t, left, right = carry
+        b, t, left, right, tleft, tright = carry
         g = visc_ref[z] * b
         bot[z] = b
         gbot[z] = g
@@ -176,14 +176,20 @@
             right = jnp.where(lane == z + j, roll(val[:, cols - 128:], z + j + 1, 1), right)
         k = levels - 1 - z
         top[k + 1] = t
-        gtop[k + 1] = visc_ref[k] * t
+        h = visc_ref[k] * t
+        gtop[k + 1] = h
+        for j, val in ((0, h), (levels, t)):
+            t_row[0, pl.ds(k + j, 1), :] = val[:1]
+            t_row[1, pl.ds(k + j, 1), :] = val[rows - 1:]
+            tleft = jnp.where(lane == k + j, roll(val[:, :128], k + j, 1), tleft)
+            tright = jnp.where(lane == k + j, roll(val[:, cols - 128:], k + j + 1, 1), tright)
         t = t * up[jnp.maximum(k - 1, 0)]
         b = b * down[jnp.minimum(z, levels - 2)]
-        return b, t, left, right
+        return b, t, left, right, tleft, tright
 
     blank = jnp.zeros((rows, 128), jnp.float32)
-    _, _, left, right = lax.fori_loop(
-        0, levels, respond, (1.0 / (f + bed_drag * friction), 1.0 / e, blank, blank), unroll=4
+    _, _, left, right, tleft, tright = lax.fori_loop(
+        0, levels, respond, (1.0 / (f + bed_drag * friction), 1.0 / e, blank, blank, blank, blank), unroll=4
     )
 
     own = [base * slide_ref[0], base * slide_ref[1], ice * obs_ref[...], inverse, bot[levels - 1], warm_ref[...], grad_ref[...]]
@@ -206,7 +212,6 @@
     each("start", ("row", "pack", "field"))
     for k in range(1, ny):
         pl.semaphore_signal(all_in, inc=1, device_id=(ix, lax.rem(iy + k, ny)), device_id_type=MESH)
-    each("wait_recv", ("row", "pack"))
 
     row_id = lax.broadcasted_iota(jnp.int32, (rows, cols), 0)
     col_id = lax.broadcasted_iota(jnp.int32, (rows, cols), 1)
@@ -220,37 +225,58 @@
             1: jnp.where(prow == rows - 1, near(at[1], 1, 0), near(at[0], 1, 0)),
         }
 
-    packs = {side: beside(side) for side in (-1, 1)}
+    def weigh(mid, out):
+        return (
+            (0.5 * offset_weight) * mid + (0.25 * offset_weight) * out,
+            (0.25 * offset_weight) * mid + (0.5 * offset_weight / 3.0) * out,
+        )
 
     def gather(z, acc):
         acc = list(acc)
-        weights = []
-        for ref in (gtop, top):
-            mid, out = ref[z + 1], ref[z] + ref[z + 2]
-            weights.append((
-                (0.5 * offset_weight) * mid + (0.25 * offset_weight) * out,
-                (0.25 * offset_weight) * mid + (0.5 * offset_weight / 3.0) * out,
-            ))
-        for j, ref, weight in ((0, bot, weights[0]), (levels, gbot, weights[1])):
+        weights = [weigh(ref[z + 1], ref[z] + ref[z + 2]) for ref in (gtop, top)]
+        for ref, weight in ((bot, weights[0]), (gbot, weights[1])):
             mid = ref[z]
-            low = jnp.where(row_id == 0, row_recv[0, pl.ds(z + j, 1), :], near(mid, -1, 0))
-            high = jnp.where(row_id == rows - 1, row_recv[1, pl.ds(z + j, 1), :], near(mid, 1, 0))
+            low = jnp.where(row_id == 0, 0.0, near(mid, -1, 0))
+            high = jnp.where(row_id == rows - 1, 0.0, near(mid, 1, 0))
             for dx, val in ((-1, low), (0, mid), (1, high)):
-                from_left = roll(packs[-1][dx], lax.rem(128 - z - j, 128), 1)
-                from_right = roll(packs[1][dx], 127 - z - j, 1)
-                wide = lambda x: jnp.concatenate([x] * (cols // 128), axis=1)
-                sides = {
-                    -1: jnp.where(col_id == 0, wide(from_left), near(val, -1, 1)),
-                    0: val,
-                    1: jnp.where(col_id == cols - 1, wide(from_right), near(val, 1, 1)),
-                }
                 for dy in (-1, 0, 1):
                     if (dx, dy) != (0, 0):
                         d = DIRS.index((dx, dy))
-                        acc[d] = acc[d] + weight[1 if dx * dy != 0 else 0] * sides[dy]
+                        moved = val if dy == 0 else near(val, dy, 1)
+                        acc[d] = acc[d] + weight[1 if dx * dy != 0 else 0] * moved
         return tuple(acc)
 
-    coefs = lax.fori_loop(0, levels, gather, (zero,) * 8, unroll=4)
+    coefs = list(lax.fori_loop(0, levels, gather, (zero,) * 8, unroll=4))
+    for d, (dx, dy) in enumerate(DIRS):
+        if dy != 0:
+            coefs[d] = jnp.where(col_id == (0 if dy < 0 else cols - 1), 0.0, coefs[d])
+
+    layer = lax.broadcasted_iota(jnp.int32, (2 * levels, cols), 0)
+    edge_col = lax.broadcasted_iota(jnp.int32, (2 * levels, cols), 1)
+
+    def above_below(mid, index, axis):
+        low = (index == 0) | (index == levels) | (index >= 2 * levels)
+        high = (index == levels - 1) | (index >= 2 * levels - 1)
+        return jnp.where(low, 0.0, near(mid, -1, axis)) + jnp.where(high, 0.0, near(mid, 1, axis))
+
+    row_weights = [weigh(t_row[i], above_below(t_row[i], layer, 0)) for i in (0, 1)]
+    col_weights = [weigh(t, above_below(t, lane, 1)) for t in (tleft, tright)]
+    each("wait_recv", ("row", "pack"))
+    for i, dx in enumerate((-1, 1)):
+        halo = row_recv[i]
+        for dy in (-1, 0, 1):
+            d = DIRS.index((dx, dy))
+            val = halo
+            if dy != 0:
+                val = jnp.where(edge_col == (0 if dy < 0 else cols - 1), 0.0, near(halo, dy, 1))
+            part = jnp.sum(row_weights[i][1 if dy != 0 else 0] * val, axis=0, keepdims=True)
+            coefs[d] = coefs[d] + jnp.where(row_id == (0 if dx < 0 else rows - 1), part, 0.0)
+    for i, dy in enumerate((-1, 1)):
+        at = beside(dy)
+        for dx in (-1, 0, 1):
+            d = DIRS.index((dx, dy))
+            part = jnp.sum(col_weights[i][1 if dx != 0 else 0] * at[dx], axis=1, keepdims=True)
+            coefs[d] = coefs[d] + jnp.where(col_id == (0 if dy < 0 else cols - 1), part, 0.0)
     for d in range(8):
         k_send[d] = coefs[d]
     kleft, kright = pack(coefs, 0, blank, blank)
@@ -400,7 +426,7 @@
                 f32(levels, rows, cols), f32(levels, rows, cols),
                 f32(levels, rows, cols), f32(levels, rows, cols),
                 f32(levels + 2, rows, cols), f32(levels + 2, rows, cols),
-                f32(2, 2 * levels, cols), f32(2, 2 * levels, cols),
+                f32(2, 2 * levels, cols), f32(2, 2 * levels, cols), f32(2, 2 * levels, cols),
                 f32(FIELDS, rows, cols), f32(2, FIELDS, rows, cols),
                 f32(2, rows, 128), f32(6, rows, 128),
                 f32(8, rows, cols), f32(2, 8, rows, cols),

time: 25.2 us -> 23.7 us (0.940)
  Pallas kernels: 23 us -> 21.5 us
    pallas_call x1, Pallas kernels: 23 us -> 21.5 us  [on_device(): pl.pallas_call(functools.partial(kernel, nx, ny), out_shape=jax.ShapeDtyp...]
where the time goes in v3:
time: 23.7 us; the launch traced here: 23.5 us
  Pallas kernels  21.5 us (91%)
  other arithmetic  1.32 us (6%)
  between operations  0.67 us (3%)
    pallas_call x1, Pallas kernels, on_device(): pl.pallas_call(functools.partial(kernel, nx, ny), out_shape=jax.ShapeDtyp...  21.5 us
    add x1, other arithmetic, on_device(): return (warm_start + change[0], gradient + change[1])  1.32 us

profile of v3, /device:TPU:0, one launch (start us, length us, event | category | flops | bytes accessed | tf_op | source)
XLA Modules:
  0.0 23.5 jit_solution(10367176348225715624)
XLA Ops:
  0.6 0.0 copy-start.1
  0.6 0.0 copy-start
  0.7 21.5 %shard_map.95 = f32[2,8,256]{2,1,0:T(8,128)} custom-call(f32[8,256]{1,0:T(8,128)} %grad_in.1, f32[8,256]{1,0:T(8,128)} %warm_in.1, f32[32,8,256]{2,1,0:T(8,128)} %visc_in.1, f32[8,256]{1,0:T(8,128)} %fric_in.1, f32[2,8,256]{2,1,0:T(8,128)} %slide_in.1, f32[8,256]{1,0:T(8,128)} %obs_in.1, s32[8,256]{1,0:T(8,128)} %ice_in.1, s32[8,256]{1,0:T(8,128)} %ground_in.1), custom_call_target="tpu_custom_call" | custom-call | tf_op jit(solution)/shard_map/pallas_call | solution.py:419
  22.2 0.0 copy-done.1
  22.2 0.0 copy-done
  22.2 1.3 %bitcast_add_fusion = (f32[8,256]{1,0:T(8,128)}, f32[8,256]{1,0:T(8,128)}) fusion(f32[8,256]{1,0:T(8,128)S(1)} %copy-done, f32[2,8,256]{2,1,0:T(8,128)} %shard_map.95, f32[8,256]{1,0:T(8,128)S(1)} %copy-done.1), kind=kLoop, calls=%fused_computation | loop fusion | flops 4096 | bytes 49152 | tf_op jit(solution)/shard_map/add | solution.py:443
Async XLA Ops:
  0.6 21.6 %copy-start.1 = (f32[8,256]{1,0:T(8,128)S(1)}, f32[8,256]{1,0:T(8,128)}, u32[]{:S(2)}) copy-start(f32[8,256]{1,0:T(8,128)} %warm_in.1) | copy-start | bytes 24580
  0.6 21.6 %copy-start = (f32[8,256]{1,0:T(8,128)S(1)}, f32[8,256]{1,0:T(8,128)}, u32[]{:S(2)}) copy-start(f32[8,256]{1,0:T(8,128)} %grad_in.1) | copy-start | bytes 24580
